TPU v7x, 32 devices: a whole 2x2x4 slice. The times are simulated.
32 devices in a mesh: node: 8 (over y, x, core), chip: 4 (over z).
Axes of the slice: x: 2, y: 2, z: 4, core: 2. Of those that a mesh axis runs over, the one named last changes fastest.
Arguments:
- momentum: float32 [32, 128, 512], P(('node', 'chip')), may hold values from -6 to 6
- gradient: bfloat16 [32, 128, 512], P(('node', 'chip')), may hold values from -6 to 6
- indices: int32 [32, 16, 32], P(('node', 'chip')), may hold values from 0 to 4095, as said below
Outputs:
- new_momentum: float32 [32, 128, 512], P(('node', 'chip'))
- update: float32 [128, 512], replicated
Inputs may be any that keep to these rules, and one draw needn't show every extreme that they name: `indices`: the 32 entries of each row name distinct coefficients of their span, coefficient (k, l) being k * 64 + l.
All inputs are finite; a program needn't handle non-finite values.
Results may differ from a plain program's by a relative error of at most 0.0029.
Values may be sent and summed in bfloat16 or wider, within the bound.
A program may use at most 64 MiB of HBM per device.

v0:
```python
import functools
import math

import jax
import jax.numpy as jnp
import numpy as np
from jax import lax
from jax.experimental import pallas as pl
from jax.experimental.pallas import tpu as pltpu
from jax.sharding import PartitionSpec as P

SPAN = 64
LANES = 128
MESH = pl.DeviceIdType.MESH
F32 = jnp.float32
BF16 = jnp.bfloat16


def cosine_blocks(copies):
    orders = np.arange(SPAN, dtype=np.float64)
    wave, cell = orders[:, None], orders[None, :]
    factor = np.where(wave == 0, math.sqrt(1 / SPAN), math.sqrt(2 / SPAN))
    table = factor * np.cos(math.pi * (2 * cell + 1) * wave / (2 * SPAN))
    full = np.kron(np.eye(copies), table)
    high = full.astype(BF16)
    low = (full - high.astype(np.float64)).astype(BF16)
    return np.stack([high.T, low.T, high, low])


def halves(x):
    high = x.astype(BF16)
    return high, (x - high.astype(F32)).astype(BF16)


def mm(a, b):
    return lax.dot_general(a, b, (((1,), (0,)), ((), ())), preferred_element_type=F32)


def mm_nt(a, b):
    return lax.dot_general(a, b, (((1,), (1,)), ((), ())), preferred_element_type=F32)


def both_sides(blocks, left, right):
    outs = []
    for x in blocks:
        high, low = halves(x)
        y = mm(high, right[0]) + (mm(low, right[0]) + mm(high, right[1]))
        high, low = halves(y)
        outs.append(mm(left[0], high) + (mm(left[0], low) + mm(left[1], high)))
    return outs


def kernel(
    nodes, chips, topk, mom_hbm, grad_hbm, idx_hbm, cos_hbm, new_out, acc, cos,
    mom, grad, idx, box, recv, in_sem, send_sem, recv_sem,
):
    node, chip = lax.axis_index("node"), lax.axis_index("chip")
    count = nodes * chips
    rows, cols = mom.shape
    per = LANES // topk
    wide = per * SPAN
    groups = idx.shape[0] // per
    strips = cols // wide
    used = 3 * groups

    loads = [
        pltpu.make_async_copy(src, dst, in_sem.at[i])
        for i, (src, dst) in enumerate(
            (
                (idx_hbm.at[0], idx),
                (cos_hbm.at[pl.ds(0, 2)], cos.at[pl.ds(0, 2)]),
                (mom_hbm.at[0], mom),
                (grad_hbm.at[0], grad),
                (cos_hbm.at[pl.ds(2, 2)], cos.at[pl.ds(2, 2)]),
            )
        )
    ]
    for load in loads:
        load.start()

    barrier = pltpu.get_barrier_semaphore()

    high_side = 2 * chip >= chips
    half = nodes // 2 if nodes % 2 == 0 else nodes

    def plane(t):
        up = t + (chip <= t).astype(jnp.int32)
        down = chips - 1 - t
        return jnp.where(high_side, up, down - (down <= chip).astype(jnp.int32))

    def peers(visit):
        def one(to_chip, base, i):
            spot = base + i
            visit({"node": jnp.where(spot >= nodes, spot - nodes, spot), "chip": to_chip})

        for t in range(chips):
            own = t == chips - 1
            go = functools.partial(one, *((chip, node) if own else (plane(t), nodes - 1 - node)))
            if nodes <= 8:
                for i in range(1 if own else 0, nodes):
                    go(i)
            else:
                pl.loop(1 if own else 0, nodes)(go)

    peers(lambda to: pl.semaphore_signal(barrier, inc=1, device_id=to, device_id_type=MESH))

    loads[0].wait()
    slots = idx[...]
    spans = slots.shape[0]
    lane = lax.broadcasted_iota(jnp.int32, (spans, LANES), 1)
    place = lax.broadcasted_iota(jnp.int32, (spans, LANES), 0) % per
    spread = jnp.concatenate([slots] * per, axis=1)
    spread = jnp.where(lane // topk == place, spread + place * (SPAN * SPAN), 0)
    lists = [
        jnp.sum(spread[g * per:(g + 1) * per], axis=0, keepdims=True) for g in range(groups)
    ]
    wave = [(x // SPAN) % SPAN for x in lists]
    wide_pos = [(x // (SPAN * SPAN)) * SPAN + x % SPAN for x in lists]
    tall_iota = lax.broadcasted_iota(jnp.int32, (SPAN, LANES), 0)
    wide_iota = lax.broadcasted_iota(jnp.int32, (wide, LANES), 0)
    wave_hot = [(tall_iota == w).astype(F32).astype(BF16) for w in wave]
    wide_hot = [(wide_iota == w).astype(F32).astype(BF16) for w in wide_pos]

    loads[1].wait()
    tall_cos = [
        mm(cos[0, :SPAN, :SPAN], hot) + mm(cos[1, :SPAN, :SPAN], hot) for hot in wave_hot
    ]
    edge = cos.shape[-1]

    def columns(table, hot):
        pieces = [mm(table, hot[p:p + edge]).astype(BF16) for p in range(0, wide, edge)]
        return jnp.concatenate(pieces, axis=0)

    wide_high = [columns(cos[0], hot) for hot in wide_hot]
    wide_low = [columns(cos[1], hot) for hot in wide_hot]

    loads[2].wait()
    loads[3].wait()
    blended = 0.9 * mom[...] + grad[...].astype(F32)

    def part(g):
        a, s = g // strips, g % strips
        return a, s

    def region(g):
        a, s = part(g)
        return slice(a * SPAN, (a + 1) * SPAN), slice(s * wide, (s + 1) * wide)

    picked = []
    for g in range(groups):
        high, low = halves(blended[region(g)])
        sums = mm(high, wide_high[g]) + (mm(low, wide_high[g]) + mm(high, wide_low[g]))
        picked.append(jnp.sum(sums * tall_cos[g], axis=0, keepdims=True))
    payload = jnp.concatenate(
        picked + [w.astype(F32) for w in wave] + [w.astype(F32) for w in wide_pos], axis=0
    ).astype(BF16)
    me = chip * nodes + node
    box[...] = payload
    recv[me] = payload

    pl.semaphore_wait(barrier, count - 1)
    peers(
        lambda to: pltpu.make_async_remote_copy(
            src_ref=box,
            dst_ref=recv.at[me],
            send_sem=send_sem,
            recv_sem=recv_sem.at[chip, node // half],
            device_id=to,
            device_id_type=MESH,
        ).start()
    )

    for g in range(groups):
        sent_value = picked[g].astype(BF16).astype(F32)
        high, low = halves(tall_cos[g] * sent_value)
        own_part = mm_nt(high, wide_high[g]) + (
            mm_nt(low, wide_high[g]) + mm_nt(high, wide_low[g])
        )
        new_out[region(g)] = blended[region(g)] - own_part

    acc[...] = jnp.zeros_like(acc)
    batch = math.gcd(half, 8)

    tall_ids = tall_iota.astype(F32).astype(BF16)
    wide_ids = wide_iota.astype(F32).astype(BF16)
    one, zero = jnp.ones((), BF16), jnp.zeros((), BF16)

    def decode(start):
        block = recv[pl.ds(start, batch)]
        for g in range(groups):
            left, right = [], []
            for i in range(batch):
                val = block[i, g:g + 1]
                row = block[i, groups + g:groups + g + 1]
                col = block[i, 2 * groups + g:2 * groups + g + 1]
                left.append(jnp.where(tall_ids == row, val, zero))
                right.append(jnp.where(wide_ids == col, one, zero))
            a, s = part(g)
            acc[pl.ds(a * SPAN, SPAN), pl.ds(s * wide, wide)] += mm_nt(
                jnp.concatenate(left, axis=1), jnp.concatenate(right, axis=1)
            )

    for t in reversed(range(chips)):
        source = chip if t == chips - 1 else plane(t)
        for h in range(nodes // half):
            part_no = lax.rem(node // half + h, nodes // half)
            first = source * nodes + part_no * half
            own = t == chips - 1 and h == 0
            if not (own and half == 1):
                landed = recv.at[pl.ds(first, half - 1 if own else half)]
                pltpu.make_async_copy(landed, landed, recv_sem.at[source, part_no]).wait()
            if half == batch:
                decode(first)
            else:
                pl.loop(0, half // batch)(lambda i: decode(first + i * batch))

    loads[4].wait()
    sent = recv.at[pl.ds(0, count - 1)]
    pltpu.make_async_copy(sent, sent, send_sem).wait()


def finish(new_in, acc, cos, new_hbm, upd_hbm, upd, sem):
    store_new = pltpu.make_async_copy(new_in, new_hbm.at[0], sem.at[0])
    store_new.start()
    rows, cols = acc.shape
    wide = cos.shape[-1]
    strips = cols // wide
    totals = [acc[:, s * wide:(s + 1) * wide] for s in range(strips)]
    same = (
        lax.broadcasted_iota(jnp.int32, (wide, wide), 0) // SPAN
        == lax.broadcasted_iota(jnp.int32, (wide, wide), 1) // SPAN
    ).astype(F32).astype(BF16)
    left = (cos[0, :rows, :rows], cos[1, :rows, :rows])
    stores = [store_new]
    for s in range(strips):
        scales = []
        for a in range(rows // SPAN):
            power = totals[s][a * SPAN:(a + 1) * SPAN]
            power = jnp.sum((power * power).reshape(SPAN // 8, 8, wide), axis=0)
            high, low = halves(power)
            energy = jnp.sum(mm(high, same) + mm(low, same), axis=0, keepdims=True)
            scales.append(1.0 / jnp.sqrt(energy * (1.0 / (SPAN * SPAN)) + 1.0))
        field = both_sides([totals[s]], left, (cos[2], cos[3]))[0]
        cut = pl.ds(s * wide, wide)
        for a, scale in enumerate(scales):
            band = slice(a * SPAN, (a + 1) * SPAN)
            upd[band, s * wide:(s + 1) * wide] = field[band] * scale
        store = pltpu.make_async_copy(upd.at[:, cut], upd_hbm.at[:, cut], sem.at[1 + s])
        store.start()
        stores.append(store)
    for store in stores:
        store.wait()


def solution(mesh):
    nodes, chips = mesh.shape["node"], mesh.shape["chip"]

    def step(momentum, gradient, indices):
        _, rows, cols = momentum.shape
        spans, topk = indices.shape[1:]
        per = LANES // topk
        wide = per * SPAN
        used = 3 * (spans // per)
        cosines = jnp.asarray(cosine_blocks(2))
        hbm = pl.BlockSpec(memory_space=pltpu.HBM)
        vmem = pl.BlockSpec(memory_space=pltpu.VMEM)
        new_momentum, totals, tables = pl.pallas_call(
            functools.partial(kernel, nodes, chips, topk),
            out_shape=(
                pltpu.VMEM((rows, cols), F32),
                pltpu.VMEM((rows, cols), F32),
                pltpu.VMEM((4, 2 * SPAN, 2 * SPAN), BF16),
            ),
            in_specs=[hbm] * 4,
            out_specs=(vmem, vmem, vmem),
            scratch_shapes=[
                pltpu.VMEM((rows, cols), F32),
                pltpu.VMEM((rows, cols), BF16),
                pltpu.VMEM((spans, topk), jnp.int32),
                pltpu.VMEM((used, LANES), BF16),
                pltpu.VMEM((nodes * chips, used, LANES), BF16),
                pltpu.SemaphoreType.DMA((5,)),
                pltpu.SemaphoreType.DMA,
                pltpu.SemaphoreType.DMA((chips, 2)),
            ],
            compiler_params=pltpu.CompilerParams(
                collective_id=0, has_side_effects=True, vmem_limit_bytes=24 * 2**20
            ),
        )(*(pltpu.with_memory_space_constraint(x, pltpu.HBM) for x in (momentum, gradient, indices, cosines)))
        return tuple(pl.pallas_call(
            finish,
            out_shape=(
                jax.ShapeDtypeStruct((1, rows, cols), F32),
                jax.ShapeDtypeStruct((rows, cols), F32),
            ),
            in_specs=[vmem, vmem, vmem],
            out_specs=(hbm, hbm),
            scratch_shapes=[
                pltpu.VMEM((rows, cols), F32),
                pltpu.SemaphoreType.DMA((1 + cols // (2 * SPAN),)),
            ],
            compiler_params=pltpu.CompilerParams(vmem_limit_bytes=24 * 2**20),
        )(new_momentum, totals, tables))

    return jax.shard_map(
        step,
        mesh=mesh,
        in_specs=(P(("node", "chip"), None, None),) * 3,
        out_specs=(P(("node", "chip"), None, None), P()),
        check_vma=False,
    )
```

profile of v0, /device:TPU:0, one launch (start us, length us, event | category | flops | bytes accessed | tf_op | source)
XLA Modules:
  0.0 14.5 jit_solution(3963737979783887038)
XLA Ops:
  0.6 12.5 %shard_map.59 = (f32[128,512]{1,0:T(8,128)S(1)}, f32[128,512]{1,0:T(8,128)S(1)}, bf16[4,128,128]{2,1,0:T(8,128)(2,1)S(1)}) custom-call(f32[1,128,512]{2,1,0:T(8,128)} %mom_hbm.1, bf16[1,128,512]{2,1,0:T(8,128)(2,1)} %grad_hbm.1, s32[1,16,32]{2,1,0:T(8,128)} %idx_hbm.1, bf16[4,128,128]{2,1,0:T(8,128)(2,1)} %constant.2.clone.cos_hbm), custom_call_target="tpu_custom_call" | custom-call | tf_op jit(solution)/shard_map/pallas_call | solution.py:267
  13.2 1.4 %shard_map.60 = (f32[1,128,512]{2,1,0:T(8,128)}, f32[128,512]{1,0:T(8,128)}) custom-call(f32[128,512]{1,0:T(8,128)S(1)} %get-tuple-element.5.new_in, f32[128,512]{1,0:T(8,128)S(1)} %get-tuple-element.6.acc, bf16[4,128,128]{2,1,0:T(8,128)(2,1)S(1)} %get-tuple-element.7.cos), custom_call_target="tpu_custom_call" | custom-call | tf_op jit(solution)/shard_map/pallas_call | solution.py:290
where the time goes:
time: 14.7 us; the launch traced here: 14.5 us
  Pallas kernels  13.9 us (95%)
  between operations  0.64 us (4%)
    pallas_call x1, Pallas kernels, step(): pl.pallas_call(functools.partial(kernel, nodes, chips, topk), out_shape=(...  12.5 us
    pallas_call x1, Pallas kernels, step(): pl.pallas_call(finish, out_shape=(jax.ShapeDtypeStruct((1, rows, cols), F...  1.35 us

commit v1 on v0

--- a/solution.py
+++ b/solution.py
@@ -61,7 +61,8 @@
     wide = per * SPAN
     groups = idx.shape[0] // per
     strips = cols // wide
-    used = 3 * groups
+    batch = math.gcd(nodes, per)
+    turn = node % batch
 
     loads = [
         pltpu.make_async_copy(src, dst, in_sem.at[i])
@@ -80,8 +81,8 @@
 
     barrier = pltpu.get_barrier_semaphore()
 
+    half = nodes // 2 if nodes % (2 * batch) == 0 else nodes
     high_side = 2 * chip >= chips
-    half = nodes // 2 if nodes % 2 == 0 else nodes
 
     def plane(t):
         up = t + (chip <= t).astype(jnp.int32)
@@ -89,18 +90,21 @@
         return jnp.where(high_side, up, down - (down <= chip).astype(jnp.int32))
 
     def peers(visit):
-        def one(to_chip, base, i):
-            spot = base + i
-            visit({"node": jnp.where(spot >= nodes, spot - nodes, spot), "chip": to_chip})
-
-        for t in range(chips):
-            own = t == chips - 1
-            go = functools.partial(one, *((chip, node) if own else (plane(t), nodes - 1 - node)))
+        def one(to_chip, i):
+            spot = nodes - 1 - node + i
+            spot = jnp.where(spot >= nodes, spot - nodes, spot)
+
+            @pl.when((to_chip != chip) | (spot != node))
+            def _():
+                visit({"node": spot, "chip": to_chip})
+
+        for to_chip in range(chips):
+            go = functools.partial(one, to_chip)
             if nodes <= 8:
-                for i in range(1 if own else 0, nodes):
+                for i in range(nodes):
                     go(i)
             else:
-                pl.loop(1 if own else 0, nodes)(go)
+                pl.loop(0, nodes)(go)
 
     peers(lambda to: pl.semaphore_signal(barrier, inc=1, device_id=to, device_id_type=MESH))
 
@@ -110,7 +114,7 @@
     lane = lax.broadcasted_iota(jnp.int32, (spans, LANES), 1)
     place = lax.broadcasted_iota(jnp.int32, (spans, LANES), 0) % per
     spread = jnp.concatenate([slots] * per, axis=1)
-    spread = jnp.where(lane // topk == place, spread + place * (SPAN * SPAN), 0)
+    spread = jnp.where(lane // topk == (place + turn) % per, spread + place * (SPAN * SPAN), 0)
     lists = [
         jnp.sum(spread[g * per:(g + 1) * per], axis=0, keepdims=True) for g in range(groups)
     ]
@@ -151,9 +155,11 @@
         high, low = halves(blended[region(g)])
         sums = mm(high, wide_high[g]) + (mm(low, wide_high[g]) + mm(high, wide_low[g]))
         picked.append(jnp.sum(sums * tall_cos[g], axis=0, keepdims=True))
-    payload = jnp.concatenate(
-        picked + [w.astype(F32) for w in wave] + [w.astype(F32) for w in wide_pos], axis=0
-    ).astype(BF16)
+    codes = [
+        (1 + w.astype(F32) / SPAN) * jnp.exp2((x % SPAN).astype(F32) - SPAN // 2)
+        for w, x in zip(wave, lists)
+    ]
+    payload = jnp.concatenate(picked + codes, axis=0).astype(BF16)
     me = chip * nodes + node
     box[...] = payload
     recv[me] = payload
@@ -179,26 +185,37 @@
         new_out[region(g)] = blended[region(g)] - own_part
 
     acc[...] = jnp.zeros_like(acc)
-    batch = math.gcd(half, 8)
-
     tall_ids = tall_iota.astype(F32).astype(BF16)
-    wide_ids = wide_iota.astype(F32).astype(BF16)
     one, zero = jnp.ones((), BF16), jnp.zeros((), BF16)
+    blank = jnp.zeros((SPAN, LANES), BF16)
+    part_row = lax.broadcasted_iota(jnp.int32, (2 * groups, LANES), 0)
+    part_lane = lax.broadcasted_iota(jnp.int32, (2 * groups, LANES), 1) // topk
+    empty = (part_row >= groups).astype(F32)
 
     def decode(start):
-        block = recv[pl.ds(start, batch)]
+        rows = [recv[start + q].astype(F32) for q in range(batch)]
+        merged = []
+        for p in range(per):
+            m = empty
+            for q in range(batch):
+                m = jnp.where(part_lane == (p + q) % per, rows[q], m)
+            power = jnp.floor(jnp.log2(m) + 1 / SPAN / 4)
+            col = power + SPAN // 2
+            row = jnp.floor((m * jnp.exp2(-power) - 1) * SPAN + 0.5)
+            merged.append((m.astype(BF16), row.astype(BF16), col.astype(BF16)))
         for g in range(groups):
-            left, right = [], []
-            for i in range(batch):
-                val = block[i, g:g + 1]
-                row = block[i, groups + g:groups + g + 1]
-                col = block[i, 2 * groups + g:2 * groups + g + 1]
-                left.append(jnp.where(tall_ids == row, val, zero))
-                right.append(jnp.where(wide_ids == col, one, zero))
             a, s = part(g)
-            acc[pl.ds(a * SPAN, SPAN), pl.ds(s * wide, wide)] += mm_nt(
-                jnp.concatenate(left, axis=1), jnp.concatenate(right, axis=1)
-            )
+            for p in range(0, per, 2):
+                left, right = [], []
+                for val, row, col in merged[p:p + 2]:
+                    left.append(jnp.where(tall_ids == row[groups + g:groups + g + 1], val[g:g + 1], zero))
+                    right.append(jnp.where(tall_ids == col[groups + g:groups + g + 1], one, zero))
+                right = jnp.concatenate(
+                    [jnp.concatenate([right[0], blank], axis=1), jnp.concatenate([blank, right[1]], axis=1)], axis=0
+                )
+                acc[pl.ds(a * SPAN, SPAN), pl.ds(s * wide + p * SPAN, 2 * SPAN)] += mm_nt(
+                    jnp.concatenate(left, axis=1), right
+                )
 
     for t in reversed(range(chips)):
         source = chip if t == chips - 1 else plane(t)
@@ -260,7 +277,7 @@
         spans, topk = indices.shape[1:]
         per = LANES // topk
         wide = per * SPAN
-        used = 3 * (spans // per)
+        used = 2 * (spans // per)
         cosines = jnp.asarray(cosine_blocks(2))
         hbm = pl.BlockSpec(memory_space=pltpu.HBM)
         vmem = pl.BlockSpec(memory_space=pltpu.VMEM)

time: 14.7 us -> 13.3 us (0.905)
  Pallas kernels: 13.9 us -> 12.5 us
    pallas_call x1, Pallas kernels: 12.5 us -> 11.1 us  [step(): pl.pallas_call(functools.partial(kernel, nodes, chips, topk), out_shape=(...]
where the time goes in v1:
time: 13.3 us; the launch traced here: 13.1 us
  Pallas kernels  12.5 us (94%)
  between operations  0.64 us (5%)
    pallas_call x1, Pallas kernels, step(): pl.pallas_call(functools.partial(kernel, nodes, chips, topk), out_shape=(...  11.1 us
    pallas_call x1, Pallas kernels, step(): pl.pallas_call(finish, out_shape=(jax.ShapeDtypeStruct((1, rows, cols), F...  1.36 us

profile of v1, /device:TPU:0, one launch (start us, length us, event | category | flops | bytes accessed | tf_op | source)
XLA Modules:
  0.0 13.1 jit_solution(7440823886847793741)
XLA Ops:
  0.6 11.1 %shard_map.59 = (f32[128,512]{1,0:T(8,128)S(1)}, f32[128,512]{1,0:T(8,128)S(1)}, bf16[4,128,128]{2,1,0:T(8,128)(2,1)S(1)}) custom-call(f32[1,128,512]{2,1,0:T(8,128)} %mom_hbm.1, bf16[1,128,512]{2,1,0:T(8,128)(2,1)} %grad_hbm.1, s32[1,16,32]{2,1,0:T(8,128)} %idx_hbm.1, bf16[4,128,128]{2,1,0:T(8,128)(2,1)} %constant.2.clone.cos_hbm), custom_call_target="tpu_custom_call" | custom-call | tf_op jit(solution)/shard_map/pallas_call | solution.py:284
  11.8 1.4 %shard_map.60 = (f32[1,128,512]{2,1,0:T(8,128)}, f32[128,512]{1,0:T(8,128)}) custom-call(f32[128,512]{1,0:T(8,128)S(1)} %get-tuple-element.5.new_in, f32[128,512]{1,0:T(8,128)S(1)} %get-tuple-element.6.acc, bf16[4,128,128]{2,1,0:T(8,128)(2,1)S(1)} %get-tuple-element.7.cos), custom_call_target="tpu_custom_call" | custom-call | tf_op jit(solution)/shard_map/pallas_call | solution.py:307

commit v2 on v1

v2 whole, which is shorter than its diff:
```python
import functools
import math

import jax
import jax.numpy as jnp
import numpy as np
from jax import lax
from jax.experimental import pallas as pl
from jax.experimental.pallas import tpu as pltpu
from jax.sharding import PartitionSpec as P

SPAN = 64
LANES = 128
MESH = pl.DeviceIdType.MESH
F32 = jnp.float32
BF16 = jnp.bfloat16


def cosine_tables():
    orders = np.arange(SPAN, dtype=np.float64)
    wave, cell = orders[:, None], orders[None, :]
    factor = np.where(wave == 0, math.sqrt(1 / SPAN), math.sqrt(2 / SPAN))
    table = factor * np.cos(math.pi * (2 * cell + 1) * wave / (2 * SPAN))
    high = table.astype(BF16)
    low = (table - high.astype(np.float64)).astype(BF16)
    pair = np.eye(LANES // SPAN, dtype=BF16)
    right = np.concatenate([np.kron(pair, high), np.kron(pair, low)], axis=1)
    left = np.concatenate([high.T, high.T, low.T, np.zeros_like(low)], axis=1)
    pick = np.pad(np.concatenate([high.T, low.T], axis=0), ((0, 0), (0, LANES - SPAN)))
    return pick, np.concatenate([right, right], axis=0), left


def halves(x):
    high = x.astype(BF16)
    return high, (x - high.astype(F32)).astype(BF16)


def mm(a, b):
    return lax.dot_general(a, b, (((1,), (0,)), ((), ())), preferred_element_type=F32)


def mm_nt(a, b):
    return lax.dot_general(a, b, (((1,), (1,)), ((), ())), preferred_element_type=F32)


def kernel(
    nodes, chips, topk, mom_hbm, grad_hbm, idx_hbm, pick_hbm, right_hbm, left_hbm, new_out, acc,
    right_cos, left_cos, pick, mom, grad, idx, box, recv, in_sem, send_sem, recv_sem,
):
    node, chip = lax.axis_index("node"), lax.axis_index("chip")
    count = nodes * chips
    rows, cols = mom.shape
    per = LANES // topk
    wide = per * SPAN
    groups = idx.shape[0] // per
    strips = cols // wide
    batch = math.gcd(nodes, per)
    turn = node % batch

    bands = rows // SPAN
    loads = [(idx_hbm.at[0], idx), (pick_hbm, pick)]
    for a in range(bands):
        band = pl.ds(a * SPAN, SPAN)
        loads += [(mom_hbm.at[0, band], mom.at[band]), (grad_hbm.at[0, band], grad.at[band])]
    loads += [(right_hbm, right_cos), (left_hbm, left_cos)]
    loads = [pltpu.make_async_copy(*x, in_sem.at[i]) for i, x in enumerate(loads)]
    for load in loads[:-2]:
        load.start()

    barrier = pltpu.get_barrier_semaphore()

    unit = 2 * batch if nodes % (2 * batch) == 0 else batch
    high_side = 2 * chip >= chips

    def plane(t):
        up = t + (chip <= t).astype(jnp.int32)
        down = chips - 1 - t
        return jnp.where(high_side, up, down - (down <= chip).astype(jnp.int32))

    def peers(visit):
        def one(to_chip, i):
            spot = nodes - 1 - node + i
            spot = jnp.where(spot >= nodes, spot - nodes, spot)

            @pl.when((to_chip != chip) | (spot != node))
            def _():
                visit({"node": spot, "chip": to_chip})

        for to_chip in range(chips):
            go = functools.partial(one, to_chip)
            if nodes <= 8:
                for i in range(nodes):
                    go(i)
            else:
                pl.loop(0, nodes)(go)

    def greet(to_chip, spot):
        pl.semaphore_signal(
            barrier, inc=1, device_id={"node": spot, "chip": to_chip}, device_id_type=MESH
        )

    def greet_own(i):
        spot = node + i
        greet(chip, jnp.where(spot >= nodes, spot - nodes, spot))

    for to_chip in map(plane, range(chips - 1)):
        if nodes <= 8:
            for spot in range(nodes):
                greet(to_chip, spot)
        else:
            pl.loop(0, nodes)(functools.partial(greet, to_chip))
    if nodes <= 8:
        for i in range(1, nodes):
            greet_own(i)
    else:
        pl.loop(1, nodes)(greet_own)

    loads[0].wait()
    slots = idx[...]
    spans = slots.shape[0]
    lane = lax.broadcasted_iota(jnp.int32, (spans, LANES), 1)
    place = lax.broadcasted_iota(jnp.int32, (spans, LANES), 0) % per
    spread = jnp.concatenate([slots] * per, axis=1)
    spread = jnp.where(lane // topk == (place + turn) % per, spread + place * (SPAN * SPAN), 0)
    lists = [
        jnp.sum(spread[g * per:(g + 1) * per], axis=0, keepdims=True) for g in range(groups)
    ]
    one, zero = jnp.ones((), BF16), jnp.zeros((), BF16)
    tall_ids = lax.broadcasted_iota(jnp.int32, (SPAN, LANES), 0).astype(F32).astype(BF16)
    wave = [((x // SPAN) % SPAN).astype(F32) for x in lists]
    cell = [(x % SPAN).astype(F32) for x in lists]
    hot = [jnp.where(tall_ids == x.astype(BF16), one, zero) for x in cell + wave]

    loads[1].wait()
    found = mm(pick[:, :SPAN], jnp.concatenate(hot, axis=1))
    found = [found[:, g * LANES:(g + 1) * LANES] for g in range(2 * groups)]
    tall_cos = [x[:SPAN] + x[SPAN:] for x in found[groups:]]
    seat = (lax.broadcasted_iota(jnp.int32, (SPAN, LANES), 1) // topk + per - turn) % per

    def columns(x):
        x = x.astype(BF16)
        return jnp.concatenate([jnp.where(seat == p, x, zero) for p in range(per)], axis=0)

    wide_high = [columns(x[:SPAN]) for x in found[:groups]]
    wide_low = [columns(x[SPAN:]) for x in found[:groups]]

    blended, picked = [], []
    for load in loads[2:-2]:
        load.wait()
    for a in range(bands):
        band = slice(a * SPAN, (a + 1) * SPAN)
        for b in range(strips):
            g = a * strips + b
            strip = slice(b * wide, (b + 1) * wide)
            blended.append(0.9 * mom[band, strip] + grad[band, strip].astype(F32))
            sums = mm(
                jnp.concatenate(halves(blended[g]), axis=0),
                jnp.concatenate([wide_high[g], wide_low[g]], axis=1),
            )
            sums = sums[:SPAN, :LANES] + (sums[SPAN:, :LANES] + sums[:SPAN, LANES:])
            picked.append(jnp.sum(sums * tall_cos[g], axis=0, keepdims=True))
    codes = [(1 + w / SPAN) * jnp.exp2(c - SPAN // 2) for w, c in zip(wave, cell)]
    payload = jnp.concatenate(picked + codes, axis=0).astype(BF16)
    me = chip * nodes + node
    box[...] = payload
    recv[me] = payload

    pl.semaphore_wait(barrier, count - 1)
    peers(
        lambda to: pltpu.make_async_remote_copy(
            src_ref=box,
            dst_ref=recv.at[me],
            send_sem=send_sem,
            recv_sem=recv_sem.at[chip],
            device_id=to,
            device_id_type=MESH,
        ).start()
    )

    for load in loads[-2:]:
        load.start()

    for g in range(groups):
        sent_value = picked[g].astype(BF16).astype(F32)
        high, low = halves(tall_cos[g] * sent_value)
        own_part = mm_nt(high, wide_high[g]) + (
            mm_nt(low, wide_high[g]) + mm_nt(high, wide_low[g])
        )
        a, b = g // strips, g % strips
        new_out[a * SPAN:(a + 1) * SPAN, b * wide:(b + 1) * wide] = blended[g] - own_part

    part_row = lax.broadcasted_iota(jnp.int32, (2 * groups, LANES), 0)
    part_lane = lax.broadcasted_iota(jnp.int32, (2 * groups, LANES), 1) // topk
    empty = (part_row >= groups).astype(F32)

    def entries(start):
        rows = [recv[start + q].astype(F32) for q in range(batch)]
        hots = []
        for p in range(per):
            m = empty
            for q in range(batch):
                m = jnp.where(part_lane == (p + q) % per, rows[q], m)
            power = jnp.floor(jnp.log2(m) + 1 / SPAN / 4)
            col = (power + SPAN // 2).astype(BF16)
            row = jnp.floor((m * jnp.exp2(-power) - 1) * SPAN + 0.5).astype(BF16)
            hots.append((m.astype(BF16), row, col))

        def hot(g, p):
            val, row, col = hots[p]
            at = groups + g
            return (
                jnp.where(tall_ids == row[at:at + 1], val[g:g + 1], zero),
                jnp.where(tall_ids == col[at:at + 1], one, zero),
            )

        return hot

    def decode(start, totals):
        hots = [entries(start + i) for i in range(0, unit, batch)]
        sums = []
        for c in range(spans):
            left, right = zip(*(hot(c // per, c % per) for hot in hots))
            sums.append(
                totals[c] + mm_nt(jnp.concatenate(left, axis=1), jnp.concatenate(right, axis=1))
            )
        return sums

    for load in loads[-2:]:
        load.wait()
    sent = recv.at[pl.ds(0, count - 1)]
    totals = [jnp.zeros((SPAN, SPAN), F32)] * spans
    for t in reversed(range(chips)):
        source = chip if t == chips - 1 else plane(t)
        first = source * nodes
        if t == 0:
            pltpu.make_async_copy(sent, sent, send_sem).wait()
        landed = recv.at[pl.ds(first, nodes - 1 if t == chips - 1 else nodes)]
        pltpu.make_async_copy(landed, landed, recv_sem.at[source]).wait()
        if unit == nodes:
            totals = decode(first, totals)
        else:
            totals = lax.fori_loop(
                0, nodes // unit, lambda i, old: decode(first + i * unit, old), totals
            )
    for c in range(0, spans, 2):
        acc[c // 2 * SPAN:(c // 2 + 1) * SPAN] = jnp.concatenate(totals[c:c + 2], axis=1)


def finish(new_in, acc, right_cos, left_cos, new_hbm, upd_hbm, upd, sem):
    store_new = pltpu.make_async_copy(new_in, new_hbm.at[0], sem.at[0])
    store_new.start()
    rows, cols = upd.shape
    strips = cols // (2 * LANES)
    turned = mm(jnp.concatenate(halves(acc[...]), axis=1), right_cos[...])
    turned = turned[:, :LANES] + turned[:, LANES:]
    pairs = acc.shape[0] // SPAN
    same = (
        lax.broadcasted_iota(jnp.int32, (LANES, LANES), 0) // SPAN
        == lax.broadcasted_iota(jnp.int32, (LANES, LANES), 1) // SPAN
    ).astype(F32).astype(BF16)
    blocks = [acc[c * SPAN:(c + 1) * SPAN] for c in range(pairs)]
    power = jnp.concatenate([jnp.sum(x * x, axis=0, keepdims=True) for x in blocks], axis=0)
    energy = mm(jnp.concatenate(halves(power), axis=0), same)
    energy = energy[:pairs] + energy[pairs:]
    scale = 1.0 / jnp.sqrt(energy * (1.0 / (SPAN * SPAN)) + 1.0)
    stores = [store_new]
    for c in range(0, pairs, 2):
        pieces = [turned[d * SPAN:(d + 1) * SPAN] for d in (c, c + 1)]
        high, low = halves(jnp.concatenate(pieces, axis=1))
        field = mm(left_cos[:, :3 * SPAN], jnp.concatenate([high, low, high], axis=0))
        level = jnp.concatenate([scale[c:c + 1], scale[c + 1:c + 2]], axis=1)
        a, s = c // 2 // strips, c // 2 % strips
        cut = pl.ds(a * SPAN, SPAN), pl.ds(s * 2 * LANES, 2 * LANES)
        upd[cut] = field * level
        store = pltpu.make_async_copy(upd.at[cut], upd_hbm.at[cut], sem.at[1 + c // 2])
        store.start()
        stores.append(store)
    for store in stores:
        store.wait()


def solution(mesh):
    nodes, chips = mesh.shape["node"], mesh.shape["chip"]

    def step(momentum, gradient, indices):
        _, rows, cols = momentum.shape
        spans, topk = indices.shape[1:]
        per = LANES // topk
        wide = per * SPAN
        used = 2 * (spans // per)
        tables = [jnp.asarray(x) for x in cosine_tables()]
        hbm = pl.BlockSpec(memory_space=pltpu.HBM)
        vmem = pl.BlockSpec(memory_space=pltpu.VMEM)
        operands = [momentum, gradient, indices, *tables]
        results = pl.pallas_call(
            functools.partial(kernel, nodes, chips, topk),
            out_shape=(
                pltpu.VMEM((rows, cols), F32),
                pltpu.VMEM((rows * cols // LANES, LANES), F32),
                *(pltpu.VMEM(x.shape, BF16) for x in tables[1:]),
            ),
            in_specs=[hbm] * 6,
            out_specs=(vmem,) * 4,
            scratch_shapes=[
                pltpu.VMEM(tables[0].shape, BF16),
                pltpu.VMEM((rows, cols), F32),
                pltpu.VMEM((rows, cols), BF16),
                pltpu.VMEM((spans, topk), jnp.int32),
                pltpu.VMEM((used, LANES), BF16),
                pltpu.VMEM((nodes * chips, used, LANES), BF16),
                pltpu.SemaphoreType.DMA((4 + 2 * (rows // SPAN),)),
                pltpu.SemaphoreType.DMA,
                pltpu.SemaphoreType.DMA((chips,)),
            ],
            compiler_params=pltpu.CompilerParams(
                collective_id=0, has_side_effects=True, vmem_limit_bytes=24 * 2**20
            ),
        )(*(pltpu.with_memory_space_constraint(x, pltpu.HBM) for x in operands))
        return tuple(pl.pallas_call(
            finish,
            out_shape=(
                jax.ShapeDtypeStruct((1, rows, cols), F32),
                jax.ShapeDtypeStruct((rows, cols), F32),
            ),
            in_specs=[vmem] * 4,
            out_specs=(hbm, hbm),
            scratch_shapes=[
                pltpu.VMEM((rows, cols), F32),
                pltpu.SemaphoreType.DMA((1 + spans // 4,)),
            ],
            compiler_params=pltpu.CompilerParams(vmem_limit_bytes=24 * 2**20),
        )(*results))

    return jax.shard_map(
        step,
        mesh=mesh,
        in_specs=(P(("node", "chip"), None, None),) * 3,
        out_specs=(P(("node", "chip"), None, None), P()),
        check_vma=False,
    )
```

time: 13.3 us -> 12.5 us (0.940)
  Pallas kernels: 12.5 us -> 11.7 us
    pallas_call x1, Pallas kernels: 11.1 us -> 10.6 us  [step(): pl.pallas_call(functools.partial(kernel, nodes, chips, topk), out_shape=(...]
    pallas_call x1, Pallas kernels: 1.36 us -> 1.12 us  [step(): pl.pallas_call(finish, out_shape=(jax.ShapeDtypeStruct((1, rows, cols), F...]
where the time goes in v2:
time: 12.5 us; the launch traced here: 12.3 us
  Pallas kernels  11.7 us (94%)
  between operations  0.64 us (5%)
    pallas_call x1, Pallas kernels, step(): pl.pallas_call(functools.partial(kernel, nodes, chips, topk), out_shape=(...  10.6 us
    pallas_call x1, Pallas kernels, step(): pl.pallas_call(finish, out_shape=(jax.ShapeDtypeStruct((1, rows, cols), F...  1.12 us

profile of v2, /device:TPU:0, one launch (start us, length us, event | category | flops | bytes accessed | tf_op | source)
XLA Modules:
  0.0 12.3 jit_solution(6308038380155142994)
XLA Ops:
  0.6 10.6 %shard_map.77 = (f32[128,512]{1,0:T(8,128)S(1)}, f32[512,128]{1,0:T(8,128)S(1)}, bf16[256,256]{1,0:T(8,128)(2,1)S(1)}, bf16[64,256]{1,0:T(8,128)(2,1)S(1)}) custom-call(f32[1,128,512]{2,1,0:T(8,128)} %mom_hbm.1, bf16[1,128,512]{2,1,0:T(8,128)(2,1)} %grad_hbm.1, s32[1,16,32]{2,1,0:T(8,128)} %idx_hbm.1, bf16[128,128]{1,0:T(8,128)(2,1)} %constant.6.clone.pick_hbm, ...), custom_call_target="tpu_custom_call" | custom-call | tf_op jit(solution)/shard_map/pallas_call | solution.py:295
  11.2 1.1 %shard_map.78 = (f32[1,128,512]{2,1,0:T(8,128)}, f32[128,512]{1,0:T(8,128)}) custom-call(f32[128,512]{1,0:T(8,128)S(1)} %get-tuple-element.6.new_in, f32[512,128]{1,0:T(8,128)S(1)} %get-tuple-element.7.acc, bf16[256,256]{1,0:T(8,128)(2,1)S(1)} %get-tuple-element.8.right_cos, bf16[64,256]{1,0:T(8,128)(2,1)S(1)} %get-tuple-element.9.left_cos), custom_call_target="tpu_custom_call" | custom-call | tf_op jit(solution)/shard_map/pallas_call | solution.py:319

commit v3 on v2

--- a/solution.py
+++ b/solution.py
@@ -44,8 +44,8 @@
 
 
 def kernel(
-    nodes, chips, topk, mom_hbm, grad_hbm, idx_hbm, pick_hbm, right_hbm, left_hbm, new_out, acc,
-    right_cos, left_cos, pick, mom, grad, idx, box, recv, in_sem, send_sem, recv_sem,
+    nodes, chips, topk, mom_hbm, grad_hbm, idx_hbm, pick_hbm, right_hbm, left_hbm, new_out, turned,
+    scale, left_cos, right_cos, pick, mom, grad, idx, box, recv, in_sem, send_sem, recv_sem,
 ):
     node, chip = lax.axis_index("node"), lax.axis_index("chip")
     count = nodes * chips
@@ -58,11 +58,14 @@
     turn = node % batch
 
     bands = rows // SPAN
-    loads = [(idx_hbm.at[0], idx), (pick_hbm, pick)]
-    for a in range(bands):
-        band = pl.ds(a * SPAN, SPAN)
-        loads += [(mom_hbm.at[0, band], mom.at[band]), (grad_hbm.at[0, band], grad.at[band])]
-    loads += [(right_hbm, right_cos), (left_hbm, left_cos)]
+    loads = [
+        (idx_hbm.at[0], idx),
+        (pick_hbm, pick),
+        (mom_hbm.at[0], mom),
+        (grad_hbm.at[0], grad),
+        (right_hbm, right_cos),
+        (left_hbm, left_cos),
+    ]
     loads = [pltpu.make_async_copy(*x, in_sem.at[i]) for i, x in enumerate(loads)]
     for load in loads[:-2]:
         load.start()
@@ -79,12 +82,9 @@
 
     def peers(visit):
         def one(to_chip, i):
-            spot = nodes - 1 - node + i
-            spot = jnp.where(spot >= nodes, spot - nodes, spot)
-
-            @pl.when((to_chip != chip) | (spot != node))
+            @pl.when((to_chip != chip) | (i != node))
             def _():
-                visit({"node": spot, "chip": to_chip})
+                visit({"node": i, "chip": to_chip})
 
         for to_chip in range(chips):
             go = functools.partial(one, to_chip)
@@ -242,29 +242,28 @@
             totals = lax.fori_loop(
                 0, nodes // unit, lambda i, old: decode(first + i * unit, old), totals
             )
-    for c in range(0, spans, 2):
-        acc[c // 2 * SPAN:(c // 2 + 1) * SPAN] = jnp.concatenate(totals[c:c + 2], axis=1)
-
-
-def finish(new_in, acc, right_cos, left_cos, new_hbm, upd_hbm, upd, sem):
-    store_new = pltpu.make_async_copy(new_in, new_hbm.at[0], sem.at[0])
-    store_new.start()
-    rows, cols = upd.shape
-    strips = cols // (2 * LANES)
-    turned = mm(jnp.concatenate(halves(acc[...]), axis=1), right_cos[...])
-    turned = turned[:, :LANES] + turned[:, LANES:]
-    pairs = acc.shape[0] // SPAN
+    pairs = [jnp.concatenate(totals[c:c + 2], axis=1) for c in range(0, spans, 2)]
+    chunk = max(1, len(pairs) // 2)
+    for c in range(0, len(pairs), chunk):
+        both = jnp.concatenate(halves(jnp.concatenate(pairs[c:c + chunk], axis=0)), axis=1)
+        both = mm(both, right_cos[...])
+        turned[c * SPAN:(c + chunk) * SPAN] = both[:, :LANES] + both[:, LANES:]
     same = (
         lax.broadcasted_iota(jnp.int32, (LANES, LANES), 0) // SPAN
         == lax.broadcasted_iota(jnp.int32, (LANES, LANES), 1) // SPAN
     ).astype(F32).astype(BF16)
-    blocks = [acc[c * SPAN:(c + 1) * SPAN] for c in range(pairs)]
-    power = jnp.concatenate([jnp.sum(x * x, axis=0, keepdims=True) for x in blocks], axis=0)
+    power = jnp.concatenate([jnp.sum(x * x, axis=0, keepdims=True) for x in pairs], axis=0)
     energy = mm(jnp.concatenate(halves(power), axis=0), same)
-    energy = energy[:pairs] + energy[pairs:]
-    scale = 1.0 / jnp.sqrt(energy * (1.0 / (SPAN * SPAN)) + 1.0)
+    energy = energy[:len(pairs)] + energy[len(pairs):]
+    scale[...] = 1.0 / jnp.sqrt(energy * (1.0 / (SPAN * SPAN)) + 1.0)
+
+
+def finish(new_in, turned, scale, left_cos, new_hbm, upd_hbm, upd, sem):
+    store_new = pltpu.make_async_copy(new_in, new_hbm.at[0], sem.at[0])
+    store_new.start()
+    strips = upd.shape[1] // (2 * LANES)
     stores = [store_new]
-    for c in range(0, pairs, 2):
+    for c in range(0, scale.shape[0], 2):
         pieces = [turned[d * SPAN:(d + 1) * SPAN] for d in (c, c + 1)]
         high, low = halves(jnp.concatenate(pieces, axis=1))
         field = mm(left_cos[:, :3 * SPAN], jnp.concatenate([high, low, high], axis=0))
@@ -297,18 +296,20 @@
             out_shape=(
                 pltpu.VMEM((rows, cols), F32),
                 pltpu.VMEM((rows * cols // LANES, LANES), F32),
-                *(pltpu.VMEM(x.shape, BF16) for x in tables[1:]),
+                pltpu.VMEM((spans // 2, LANES), F32),
+                pltpu.VMEM(tables[2].shape, BF16),
             ),
             in_specs=[hbm] * 6,
             out_specs=(vmem,) * 4,
             scratch_shapes=[
+                pltpu.VMEM(tables[1].shape, BF16),
                 pltpu.VMEM(tables[0].shape, BF16),
                 pltpu.VMEM((rows, cols), F32),
                 pltpu.VMEM((rows, cols), BF16),
                 pltpu.VMEM((spans, topk), jnp.int32),
                 pltpu.VMEM((used, LANES), BF16),
                 pltpu.VMEM((nodes * chips, used, LANES), BF16),
-                pltpu.SemaphoreType.DMA((4 + 2 * (rows // SPAN),)),
+                pltpu.SemaphoreType.DMA((6,)),
                 pltpu.SemaphoreType.DMA,
                 pltpu.SemaphoreType.DMA((chips,)),
             ],

time: 12.5 us -> 12.3 us (0.984)
  Pallas kernels: 11.7 us -> 11.5 us
    pallas_call x1, Pallas kernels: 1.12 us -> 0.91 us  [step(): pl.pallas_call(finish, out_shape=(jax.ShapeDtypeStruct((1, rows, cols), F...]
where the time goes in v3:
time: 12.3 us; the launch traced here: 12.1 us
  Pallas kernels  11.5 us (93%)
  between operations  0.64 us (5%)
    pallas_call x1, Pallas kernels, step(): pl.pallas_call(functools.partial(kernel, nodes, chips, topk), out_shape=(...  10.6 us
    pallas_call x1, Pallas kernels, step(): pl.pallas_call(finish, out_shape=(jax.ShapeDtypeStruct((1, rows, cols), F...  0.91 us

profile of v3, /device:TPU:0, one launch (start us, length us, event | category | flops | bytes accessed | tf_op | source)
XLA Modules:
  0.0 12.1 jit_solution(6895169493061064062)
XLA Ops:
  0.6 10.6 %shard_map.77 = (f32[128,512]{1,0:T(8,128)S(1)}, f32[512,128]{1,0:T(8,128)S(1)}, f32[8,128]{1,0:T(8,128)S(1)}, bf16[64,256]{1,0:T(8,128)(2,1)S(1)}) custom-call(f32[1,128,512]{2,1,0:T(8,128)} %mom_hbm.1, bf16[1,128,512]{2,1,0:T(8,128)(2,1)} %grad_hbm.1, s32[1,16,32]{2,1,0:T(8,128)} %idx_hbm.1, bf16[128,128]{1,0:T(8,128)(2,1)} %constant.6.clone.pick_hbm, ...), custom_call_target="tpu_custom_call" | custom-call | tf_op jit(solution)/shard_map/pallas_call | solution.py:294
  11.2 0.9 %shard_map.78 = (f32[1,128,512]{2,1,0:T(8,128)}, f32[128,512]{1,0:T(8,128)}) custom-call(f32[128,512]{1,0:T(8,128)S(1)} %get-tuple-element.6.new_in, f32[512,128]{1,0:T(8,128)S(1)} %get-tuple-element.7.turned, f32[8,128]{1,0:T(8,128)S(1)} %get-tuple-element.8.scale, bf16[64,256]{1,0:T(8,128)(2,1)S(1)} %get-tuple-element.9.left_cos), custom_call_target="tpu_custom_call" | custom-call | tf_op jit(solution)/shard_map/pallas_call | solution.py:320

commit v4 on v3

--- a/solution.py
+++ b/solution.py
@@ -26,7 +26,7 @@
     pair = np.eye(LANES // SPAN, dtype=BF16)
     right = np.concatenate([np.kron(pair, high), np.kron(pair, low)], axis=1)
     left = np.concatenate([high.T, high.T, low.T, np.zeros_like(low)], axis=1)
-    pick = np.pad(np.concatenate([high.T, low.T], axis=0), ((0, 0), (0, LANES - SPAN)))
+    pick = np.pad(table.T, ((0, 0), (0, LANES - SPAN))).astype(F32)
     return pick, np.concatenate([right, right], axis=0), left
 
 
@@ -45,10 +45,10 @@
 
 def kernel(
     nodes, chips, topk, mom_hbm, grad_hbm, idx_hbm, pick_hbm, right_hbm, left_hbm, new_out, turned,
-    scale, left_cos, right_cos, pick, mom, grad, idx, box, recv, in_sem, send_sem, recv_sem,
+    power, left_cos, right_cos, pick, mom, grad, idx, box, recv, in_sem, send_sem, recv_sem,
 ):
     node, chip = lax.axis_index("node"), lax.axis_index("chip")
-    count = nodes * chips
+    devices = nodes * chips
     rows, cols = mom.shape
     per = LANES // topk
     wide = per * SPAN
@@ -67,8 +67,15 @@
         (left_hbm, left_cos),
     ]
     loads = [pltpu.make_async_copy(*x, in_sem.at[i]) for i, x in enumerate(loads)]
-    for load in loads[:-2]:
+    for load in loads[:2]:
         load.start()
+    for src, dst, sem, priority, count in (
+        (mom_hbm.at[0], mom, in_sem.at[2], 1, 8),
+        (grad_hbm.at[0], grad, in_sem.at[3], 0, 4),
+    ):
+        for i in range(count):
+            cut = pl.ds(i * rows // count, rows // count)
+            pltpu.make_async_copy(src.at[cut], dst.at[cut], sem).start(priority=priority)
 
     barrier = pltpu.get_barrier_semaphore()
 
@@ -129,20 +136,21 @@
     tall_ids = lax.broadcasted_iota(jnp.int32, (SPAN, LANES), 0).astype(F32).astype(BF16)
     wave = [((x // SPAN) % SPAN).astype(F32) for x in lists]
     cell = [(x % SPAN).astype(F32) for x in lists]
-    hot = [jnp.where(tall_ids == x.astype(BF16), one, zero) for x in cell + wave]
-
     loads[1].wait()
-    found = mm(pick[:, :SPAN], jnp.concatenate(hot, axis=1))
-    found = [found[:, g * LANES:(g + 1) * LANES] for g in range(2 * groups)]
-    tall_cos = [x[:SPAN] + x[SPAN:] for x in found[groups:]]
+
+    def gather(row):
+        spots = jnp.broadcast_to(row.astype(jnp.int32), (SPAN, LANES))
+        return jnp.take_along_axis(pick[...], spots, axis=1, mode="promise_in_bounds")
+
+    found = [halves(gather(x)) for x in cell]
+    tall_cos = [gather(x) for x in wave]
     seat = (lax.broadcasted_iota(jnp.int32, (SPAN, LANES), 1) // topk + per - turn) % per
 
     def columns(x):
-        x = x.astype(BF16)
         return jnp.concatenate([jnp.where(seat == p, x, zero) for p in range(per)], axis=0)
 
-    wide_high = [columns(x[:SPAN]) for x in found[:groups]]
-    wide_low = [columns(x[SPAN:]) for x in found[:groups]]
+    wide_high = [columns(x[0]) for x in found]
+    wide_low = [columns(x[1]) for x in found]
 
     blended, picked = [], []
     for load in loads[2:-2]:
@@ -165,7 +173,7 @@
     box[...] = payload
     recv[me] = payload
 
-    pl.semaphore_wait(barrier, count - 1)
+    pl.semaphore_wait(barrier, devices - 1)
     peers(
         lambda to: pltpu.make_async_remote_copy(
             src_ref=box,
@@ -227,7 +235,7 @@
 
     for load in loads[-2:]:
         load.wait()
-    sent = recv.at[pl.ds(0, count - 1)]
+    sent = recv.at[pl.ds(0, devices - 1)]
     totals = [jnp.zeros((SPAN, SPAN), F32)] * spans
     for t in reversed(range(chips)):
         source = chip if t == chips - 1 else plane(t)
@@ -248,22 +256,23 @@
         both = jnp.concatenate(halves(jnp.concatenate(pairs[c:c + chunk], axis=0)), axis=1)
         both = mm(both, right_cos[...])
         turned[c * SPAN:(c + chunk) * SPAN] = both[:, :LANES] + both[:, LANES:]
+    power[...] = jnp.concatenate([jnp.sum(x * x, axis=0, keepdims=True) for x in pairs], axis=0)
+
+
+def finish(new_in, turned, power, left_cos, new_hbm, upd_hbm, upd, sem):
+    store_new = pltpu.make_async_copy(new_in, new_hbm.at[0], sem.at[0])
+    store_new.start()
+    strips = upd.shape[1] // (2 * LANES)
+    pairs = power.shape[0]
     same = (
         lax.broadcasted_iota(jnp.int32, (LANES, LANES), 0) // SPAN
         == lax.broadcasted_iota(jnp.int32, (LANES, LANES), 1) // SPAN
     ).astype(F32).astype(BF16)
-    power = jnp.concatenate([jnp.sum(x * x, axis=0, keepdims=True) for x in pairs], axis=0)
-    energy = mm(jnp.concatenate(halves(power), axis=0), same)
-    energy = energy[:len(pairs)] + energy[len(pairs):]
-    scale[...] = 1.0 / jnp.sqrt(energy * (1.0 / (SPAN * SPAN)) + 1.0)
-
-
-def finish(new_in, turned, scale, left_cos, new_hbm, upd_hbm, upd, sem):
-    store_new = pltpu.make_async_copy(new_in, new_hbm.at[0], sem.at[0])
-    store_new.start()
-    strips = upd.shape[1] // (2 * LANES)
+    energy = mm(jnp.concatenate(halves(power[...]), axis=0), same)
+    energy = energy[:pairs] + energy[pairs:]
+    scale = 1.0 / jnp.sqrt(energy * (1.0 / (SPAN * SPAN)) + 1.0)
     stores = [store_new]
-    for c in range(0, scale.shape[0], 2):
+    for c in range(0, pairs, 2):
         pieces = [turned[d * SPAN:(d + 1) * SPAN] for d in (c, c + 1)]
         high, low = halves(jnp.concatenate(pieces, axis=1))
         field = mm(left_cos[:, :3 * SPAN], jnp.concatenate([high, low, high], axis=0))
@@ -303,7 +312,7 @@
             out_specs=(vmem,) * 4,
             scratch_shapes=[
                 pltpu.VMEM(tables[1].shape, BF16),
-                pltpu.VMEM(tables[0].shape, BF16),
+                pltpu.VMEM(tables[0].shape, F32),
                 pltpu.VMEM((rows, cols), F32),
                 pltpu.VMEM((rows, cols), BF16),
                 pltpu.VMEM((spans, topk), jnp.int32),

time: 12.3 us -> 12.3 us (level)
  no operation moved by 1% of the time
where the time goes in v4:
time: 12.3 us; the launch traced here: 12.1 us
  Pallas kernels  11.5 us (93%)
  between operations  0.64 us (5%)
    pallas_call x1, Pallas kernels, step(): pl.pallas_call(functools.partial(kernel, nodes, chips, topk), out_shape=(...  10.6 us
    pallas_call x1, Pallas kernels, step(): pl.pallas_call(finish, out_shape=(jax.ShapeDtypeStruct((1, rows, cols), F...  0.9 us

profile of v4, /device:TPU:0, one launch (start us, length us, event | category | flops | bytes accessed | tf_op | source)
XLA Modules:
  0.0 12.1 jit_solution(13594750952922600362)
XLA Ops:
  0.6 10.6 %shard_map.77 = (f32[128,512]{1,0:T(8,128)S(1)}, f32[512,128]{1,0:T(8,128)S(1)}, f32[8,128]{1,0:T(8,128)S(1)}, bf16[64,256]{1,0:T(8,128)(2,1)S(1)}) custom-call(f32[1,128,512]{2,1,0:T(8,128)} %mom_hbm.1, bf16[1,128,512]{2,1,0:T(8,128)(2,1)} %grad_hbm.1, s32[1,16,32]{2,1,0:T(8,128)} %idx_hbm.1, f32[64,128]{1,0:T(8,128)} %constant.6.clone.pick_hbm, ...), custom_call_target="tpu_custom_call" | custom-call | tf_op jit(solution)/shard_map/pallas_call | solution.py:303
  11.2 0.9 %shard_map.78 = (f32[1,128,512]{2,1,0:T(8,128)}, f32[128,512]{1,0:T(8,128)}) custom-call(f32[128,512]{1,0:T(8,128)S(1)} %get-tuple-element.6.new_in, f32[512,128]{1,0:T(8,128)S(1)} %get-tuple-element.7.turned, f32[8,128]{1,0:T(8,128)S(1)} %get-tuple-element.8.power, bf16[64,256]{1,0:T(8,128)(2,1)S(1)} %get-tuple-element.9.left_cos), custom_call_target="tpu_custom_call" | custom-call | tf_op jit(solution)/shard_map/pallas_call | solution.py:329
